TPU v7x, 128 devices: a whole 4x4x4 slice. The times are simulated.
128 devices in a mesh: seq: 8 (over z, core), grp: 16 (over y, x).
Axes of the slice: x: 4, y: 4, z: 4, core: 2. Of those that a mesh axis runs over, the one named last changes fastest.
Arguments:
- hidden_in: bfloat16 [16, 4096, 1024], P('grp', 'seq'), may hold values from -64 to 64, as said below
- lengths: int32 [16], P('grp'), may hold values from 512 to 4096
- project_weight: bfloat16 [1024, 3072], replicated, may hold values from -0.1875 to 0.1875
- output_weight: bfloat16 [1024, 1024], replicated, may hold values from -0.1875 to 0.1875
- first_gain: float32 [1024], replicated, may hold values from 0.5 to 1.5
- first_shift: float32 [1024], replicated, may hold values from -3 to 3
- up_weight: bfloat16 [1024, 4096], P('grp'), may hold values from -0.1875 to 0.1875
- down_weight: bfloat16 [1024, 4096], P('grp'), may hold values from -0.09375 to 0.09375
- second_gain: float32 [1024], replicated, may hold values from 0.5 to 1.5
- second_shift: float32 [1024], replicated, may hold values from -3 to 3
- queries: float32 [128, 1024], P('grp'), may hold values from -6 to 6
- positive: int32 [128], P('grp'), may hold values from 0 to 15
Outputs:
- hidden_out: bfloat16 [16, 4096, 1024], P('grp', 'seq')
- embeddings: float32 [16, 1024], P('grp')
- query_loss: float32 [128], P('grp')
Inputs may be any that keep to these rules, and one draw needn't show every extreme that they name: `hidden_in`: activations.
All inputs are finite; a program needn't handle non-finite values.
Results may differ from a plain program's by a relative error of at most 0.0076.
Values may be sent and summed in bfloat16 or wider, within the bound.
A program may use at most 192 MiB of HBM per device.

v0:
```python
import math
import jax
import jax.numpy as jnp
from jax import lax
from jax.sharding import PartitionSpec as P

HEAD_DIM = 64


def sent_together(arrays, axis, dim, along):
    widths = [a.shape[along] for a in arrays]
    both = jnp.concatenate(arrays, axis=along)
    result = lax.all_gather(both, axis, axis=dim, tiled=True)
    return tuple(jnp.split(result, [sum(widths[:k]) for k in range(1, len(widths))], axis=along))


def split_up(array, dim, devices):
    before, after = (array.shape[:dim], array.shape[dim + 1 :])
    return jnp.moveaxis(array.reshape(*before, devices, -1, *after), dim, 0)


def cut_rows(length, count):
    unit = 8 if length >= 8 * count else 1
    return [length // unit * k // count * unit for k in range(1, count)]


def laid_out(parts, dim):
    lengths = list(parts.shape[1:])
    lengths[dim] *= parts.shape[0]
    return jnp.moveaxis(parts, 0, dim).reshape(lengths)


def several_exchanges(array, axis, pieces, split_dim, concat_dim):
    parts = split_up(array, split_dim, lax.axis_size(axis))
    cut = max(range(1, max(2, parts.ndim - 1)), key=lambda d: parts.shape[d])
    outs = []
    for slab in jnp.split(parts, cut_rows(parts.shape[cut], pieces), axis=cut):
        if slab.size:
            outs.append(lax.all_to_all(slab, axis, split_axis=0, concat_axis=0, tiled=True))
    return laid_out(jnp.concatenate(outs, axis=cut), concat_dim)


def sent_to_all(array, axis):
    copies = jnp.broadcast_to(array, (lax.axis_size(axis), *array.shape))
    return lax.all_to_all(copies, axis, split_axis=0, concat_axis=0, tiled=True)


def taken_together(array, axis):
    everything = sent_to_all(array, axis)
    return jnp.sum(everything, axis=0)


def collect(array, axis, dim):
    parts = sent_to_all(array, axis)
    return laid_out(parts, dim)


def layer_norm(values, gain, shift):
    average = jnp.mean(values, axis=-1, keepdims=True)
    centred = values - average
    variance = jnp.mean(centred * centred, axis=-1, keepdims=True)
    return centred * lax.rsqrt(variance + 1e-05) * gain + shift


def attend_local(gathered, length):
    seq_len = gathered.shape[0]
    local_width = gathered.shape[2]
    head_count = local_width // HEAD_DIM
    block = min(1024, seq_len)
    query_all = gathered[:, 0, :].reshape(seq_len, head_count, HEAD_DIM)
    key_all = gathered[:, 1, :].reshape(seq_len, head_count, HEAD_DIM)
    value_all = gathered[:, 2, :].reshape(seq_len, head_count, HEAD_DIM)
    key_valid = jnp.arange(seq_len, dtype=jnp.int32) < length
    scale = 1.0 / math.sqrt(HEAD_DIM)

    def one_block(index):
        query_rows = lax.dynamic_slice_in_dim(query_all, index * block, block, 0)
        scores = (
            jnp.einsum("qhd,khd->hqk", query_rows, key_all, preferred_element_type=jnp.float32)
            * scale
        )
        scores = jnp.where(key_valid[None, None, :], scores, -jnp.inf)
        highest = jnp.max(scores, axis=-1, keepdims=True)
        expo = jnp.exp(scores - highest)
        probs = (expo / jnp.sum(expo, axis=-1, keepdims=True)).astype(jnp.bfloat16)
        result = jnp.einsum("hqk,khd->qhd", probs, value_all, preferred_element_type=jnp.float32)
        return result.astype(jnp.bfloat16).reshape(block, local_width)

    blocks = lax.map(one_block, jnp.arange(seq_len // block, dtype=jnp.int32))
    return blocks.reshape(seq_len, local_width)


def group_weights(up_part, down_part):
    return sent_together((up_part, down_part), "grp", 0, 1)


def expand_inner(rows_in, up_full):
    return jax.nn.gelu(
        jnp.dot(rows_in, up_full, preferred_element_type=jnp.float32), approximate=False
    ).astype(jnp.bfloat16)


def contract_down(inner_rows, down_full):
    return lax.dot_general(
        inner_rows, down_full, (((1,), (1,)), ((), ())), preferred_element_type=jnp.float32
    )


def body(
    hidden_in,
    lengths,
    project_weight,
    output_weight,
    first_gain,
    first_shift,
    up_weight,
    down_weight,
    second_gain,
    second_shift,
    queries,
    positive,
):
    tokens = hidden_in[0]
    tok_rows = tokens.shape[0]
    width = tokens.shape[1]
    rank = lax.axis_index("seq")
    length = lengths[0]
    projected = jnp.dot(tokens, project_weight, preferred_element_type=jnp.float32).astype(
        jnp.bfloat16
    )
    projected = projected.reshape(tok_rows, 3, width)
    gathered = several_exchanges(projected, "seq", 2, 2, 0)
    attended = attend_local(gathered, length)
    returned = lax.all_to_all(attended, "seq", split_axis=0, concat_axis=1, tiled=True)
    mixed = jnp.dot(returned, output_weight, preferred_element_type=jnp.float32)
    mixed = mixed + tokens.astype(jnp.float32)
    normed = layer_norm(mixed, first_gain, first_shift).astype(jnp.bfloat16)
    up_full, down_full = group_weights(up_weight, down_weight)
    inner = expand_inner(normed, up_full)
    outer = contract_down(inner, down_full)
    final = layer_norm(outer + normed.astype(jnp.float32), second_gain, second_shift)
    position = rank * tok_rows + jnp.arange(tok_rows, dtype=jnp.int32)
    valid = (position < length).astype(jnp.float32)
    local_total = jnp.sum(final * valid[:, None], axis=0)
    passage_total = taken_together(local_total, "seq")
    pooled = passage_total / length.astype(jnp.float32)
    embedding = pooled / jnp.sqrt(jnp.sum(pooled * pooled) + 1e-06)
    short_passages = collect(embedding.astype(jnp.bfloat16)[None, :], "grp", 0)
    short_queries = (
        queries / jnp.sqrt(jnp.sum(queries * queries, axis=-1, keepdims=True) + 1e-06)
    ).astype(jnp.bfloat16)
    logits = 20.0 * jnp.dot(short_queries, short_passages.T, preferred_element_type=jnp.float32)
    passage_ids = jnp.arange(short_passages.shape[0], dtype=jnp.int32)
    chosen = positive[:, None] == passage_ids[None, :]
    picked = jnp.sum(jnp.where(chosen, logits, 0.0), axis=1)
    query_loss = jnp.log(jnp.sum(jnp.exp(logits), axis=1)) - picked
    return (final.astype(jnp.bfloat16)[None], embedding[None, :], query_loss)


def solution(mesh):
    in_specs = (
        P("grp", "seq", None),
        P("grp"),
        P(),
        P(),
        P(),
        P(),
        P("grp", None),
        P("grp", None),
        P(),
        P(),
        P("grp", None),
        P("grp"),
    )
    out_specs = (P("grp", "seq", None), P("grp", None), P("grp"))
    return jax.shard_map(body, mesh=mesh, in_specs=in_specs, out_specs=out_specs, check_vma=False)
```

profile of v0, /device:TPU:0, one launch (start us, length us, event | category | flops | bytes accessed | tf_op | source)
XLA Modules:
  0.0 313.7 jit_solution(6332534830161004990)
XLA Ops:
  7.2 0.0 all-gather.2.cloned.1.call-start
  7.2 2.4 pad_maximum_fusion.1
  9.6 6.6 %fusion.69 = bf16[64,8,24,128]{3,1,2,0:T(8,128)(2,1)S(1)} fusion(bf16[1024,3072]{1,0:T(8,128)(2,1)} %param.16, bf16[1,512,1024]{2,1,0:T(8,128)(2,1)} %param.14), kind=kOutput, calls=%fused_computation.84 | convolution fusion | flops 3222798336 | bytes 10485760 | tf_op jit(solution)/shard_map/dot_general | solution.py:128
  16.2 0.9 copy.57
  17.1 0.7 copy.65
  17.7 1.5 fusion.130
  19.3 26.9 %all_to_all.40 = bf16[8,256,3,128]{3,1,2,0:T(8,128)(2,1)} all-to-all(bf16[8,256,3,128]{3,1,2,0:T(8,128)(2,1)S(1)} %get-tuple-element.88), channel_id=1, replica_groups=mesh['seq'=8,'grp'=16] {'seq'}, dimensions={0} | all-to-all | bytes 3145728 | tf_op jit(solution)/shard_map/all_to_all | solution.py:39
  46.2 4.5 %all-to-all-start.1 = ((bf16[8,256,3,128]{3,1,2,0:T(8,128)(2,1)}), bf16[8,256,3,128]{3,1,2,0:T(8,128)(2,1)}, u32[]{:S(2)}, u32[]{:S(2)}) async-start(bf16[8,256,3,128]{3,1,2,0:T(8,128)(2,1)} %get-tuple-element.89), calls=%async_computation.1 | async-start | bytes 3145728 | tf_op jit(solution)/shard_map/all_to_all | solution.py:39
  50.6 21.4 %all-to-all-done.1 = bf16[8,256,3,128]{3,1,2,0:T(8,128)(2,1)} async-done(((bf16[8,256,3,128]{3,1,2,0:T(8,128)(2,1)}), bf16[8,256,3,128]{3,1,2,0:T(8,128)(2,1)}, u32[]{:S(2)}, u32[]{:S(2)}) %all-to-all-start.1) | async-done | bytes 1572896 | tf_op jit(solution)/shard_map/all_to_all | solution.py:39
  72.0 2.2 pad_maximum_fusion
  74.2 0.3 copy.52
  74.5 1.6 fusion.129
  76.1 2.3 copy.46
  78.4 2.3 copy.47
  80.7 1.3 copy.48
  82.0 134.7 %while.11 = (s32[]{:T(128)}, bf16[4,1024,128]{2,1,0:T(8,128)(2,1)}, s32[4]{0:T(128)S(1)}, bf16[4096,2,64]{0,2,1:T(8,128)(2,1)}, bf16[4096,2,64]{0,2,1:T(8,128)(2...) while((s32[]{:T(128)}, bf16[4,1024,128]{2,1,0:T(8,128)(2,1)}, ...), condition=%wide.region_3.4_spmd.clone, body=%wide.region_0.3_spmd.clone.sunk | while | flops 2197954560 | bytes 70804144 | solution.py:89
  82.0 0.6 dynamic_slice.24
  83.2 0.7 iota_compare_fusion.3
  83.9 17.5 %fusion.154 = (f32[2,1024]{1,0:T(2,128)S(1)}, f32[2,1024,4096]{2,1,0:T(8,128)}) fusion(pred[4096]{0:T(1024)(128)(4,1)S(1)} %iota_compare_fusion.3, bf16[4096,2,64]{0,2,1:T(8,128)(2,1)} %get-tuple-element.169, bf16[4096,2,64]{0,2,1:T(8,128)(2,1)} %get-tuple-element.168, s32[]{:T(128)S(6)} %select_n.28), kind=kOutput, calls=%fused_computation.143.clone.1 | convolution fusion | flops 1107300352 | bytes 34877444 | tf_op jit(solution)/shard_map/while/body/eval_jaxpr/sub | solution.py:84
  101.4 13.9 %fusion.155 = bf16[2,1024,64]{1,2,0:T(8,128)(2,1)S(1)} fusion(bf16[4096,2,64]{0,2,1:T(8,128)(2,1)} %get-tuple-element.170, f32[2,1024,4096]{2,1,0:T(8,128)} %get-tuple-element.141, f32[2,1024]{1,0:T(2,128)S(1)} %get-tuple-element.142), kind=kOutput, calls=%fused_computation.11.clone.1 | convolution fusion | flops 1090650112 | bytes 34873344 | tf_op jit(solution)/shard_map/while/body/eval_jaxpr/hqk,khd->qhd/dot_general | solution.py:86
  115.3 0.2 copy.67
  115.5 0.7 constant_dynamic-update-slice_fusion.2
  116.2 0.6 dynamic_slice.24
  117.5 0.7 iota_compare_fusion.3
  118.1 17.1 %fusion.154 = (f32[2,1024]{1,0:T(2,128)S(1)}, f32[2,1024,4096]{2,1,0:T(8,128)}) fusion(pred[4096]{0:T(1024)(128)(4,1)S(1)} %iota_compare_fusion.3, bf16[4096,2,64]{0,2,1:T(8,128)(2,1)} %get-tuple-element.169, bf16[4096,2,64]{0,2,1:T(8,128)(2,1)} %get-tuple-element.168, s32[]{:T(128)S(6)} %select_n.28), kind=kOutput, calls=%fused_computation.143.clone.1 | convolution fusion | flops 1107300352 | bytes 34877444 | tf_op jit(solution)/shard_map/while/body/eval_jaxpr/sub | solution.py:84
  135.2 13.6 %fusion.155 = bf16[2,1024,64]{1,2,0:T(8,128)(2,1)S(1)} fusion(bf16[4096,2,64]{0,2,1:T(8,128)(2,1)} %get-tuple-element.170, f32[2,1024,4096]{2,1,0:T(8,128)} %get-tuple-element.141, f32[2,1024]{1,0:T(2,128)S(1)} %get-tuple-element.142), kind=kOutput, calls=%fused_computation.11.clone.1 | convolution fusion | flops 1090650112 | bytes 34873344 | tf_op jit(solution)/shard_map/while/body/eval_jaxpr/hqk,khd->qhd/dot_general | solution.py:86
  148.8 0.2 copy.67
  149.0 0.7 constant_dynamic-update-slice_fusion.2
  149.7 0.6 dynamic_slice.24
  151.0 0.7 iota_compare_fusion.3
  151.6 17.1 %fusion.154 = (f32[2,1024]{1,0:T(2,128)S(1)}, f32[2,1024,4096]{2,1,0:T(8,128)}) fusion(pred[4096]{0:T(1024)(128)(4,1)S(1)} %iota_compare_fusion.3, bf16[4096,2,64]{0,2,1:T(8,128)(2,1)} %get-tuple-element.169, bf16[4096,2,64]{0,2,1:T(8,128)(2,1)} %get-tuple-element.168, s32[]{:T(128)S(6)} %select_n.28), kind=kOutput, calls=%fused_computation.143.clone.1 | convolution fusion | flops 1107300352 | bytes 34877444 | tf_op jit(solution)/shard_map/while/body/eval_jaxpr/sub | solution.py:84
  168.7 13.6 %fusion.155 = bf16[2,1024,64]{1,2,0:T(8,128)(2,1)S(1)} fusion(bf16[4096,2,64]{0,2,1:T(8,128)(2,1)} %get-tuple-element.170, f32[2,1024,4096]{2,1,0:T(8,128)} %get-tuple-element.141, f32[2,1024]{1,0:T(2,128)S(1)} %get-tuple-element.142), kind=kOutput, calls=%fused_computation.11.clone.1 | convolution fusion | flops 1090650112 | bytes 34873344 | tf_op jit(solution)/shard_map/while/body/eval_jaxpr/hqk,khd->qhd/dot_general | solution.py:86
  182.3 0.2 copy.67
  182.5 0.7 constant_dynamic-update-slice_fusion.2
  183.2 0.6 dynamic_slice.24
  184.5 0.7 iota_compare_fusion.3
  185.1 17.1 %fusion.154 = (f32[2,1024]{1,0:T(2,128)S(1)}, f32[2,1024,4096]{2,1,0:T(8,128)}) fusion(pred[4096]{0:T(1024)(128)(4,1)S(1)} %iota_compare_fusion.3, bf16[4096,2,64]{0,2,1:T(8,128)(2,1)} %get-tuple-element.169, bf16[4096,2,64]{0,2,1:T(8,128)(2,1)} %get-tuple-element.168, s32[]{:T(128)S(6)} %select_n.28), kind=kOutput, calls=%fused_computation.143.clone.1 | convolution fusion | flops 1107300352 | bytes 34877444 | tf_op jit(solution)/shard_map/while/body/eval_jaxpr/sub | solution.py:84
  202.2 13.6 %fusion.155 = bf16[2,1024,64]{1,2,0:T(8,128)(2,1)S(1)} fusion(bf16[4096,2,64]{0,2,1:T(8,128)(2,1)} %get-tuple-element.170, f32[2,1024,4096]{2,1,0:T(8,128)} %get-tuple-element.141, f32[2,1024]{1,0:T(2,128)S(1)} %get-tuple-element.142), kind=kOutput, calls=%fused_computation.11.clone.1 | convolution fusion | flops 1090650112 | bytes 34873344 | tf_op jit(solution)/shard_map/while/body/eval_jaxpr/hqk,khd->qhd/dot_general | solution.py:86
  215.8 0.2 copy.67
  216.0 0.7 constant_dynamic-update-slice_fusion.2
  216.7 3.7 %all-to-all-start.2 = ((bf16[8,512,128]{2,1,0:T(8,128)(2,1)}), bf16[8,512,128]{2,1,0:T(8,128)(2,1)S(1)}, u32[]{:S(2)}, u32[]{:S(2)}) async-start(bf16[8,512,128]{2,1,0:T(8,128)(2,1)} %bitcast.57), calls=%async_computation.2 | async-start | bytes 2097152 | tf_op jit(solution)/shard_map/all_to_all | solution.py:134
  221.1 15.2 %all-to-all-done.2 = bf16[8,512,128]{2,1,0:T(8,128)(2,1)S(1)} async-done(((bf16[8,512,128]{2,1,0:T(8,128)(2,1)}), bf16[8,512,128]{2,1,0:T(8,128)(2,1)S(1)}, u32[]{:S(2)}, u32[]{:S(2)}) %all-to-all-start.2) | async-done | bytes 1048608 | tf_op jit(solution)/shard_map/all_to_all | solution.py:134
  236.3 1.3 copy.50
  237.6 2.9 fusion.131
  240.5 1.3 copy-done.1
  241.8 0.3 multiply_reduce_fusion.2
  242.2 0.0 all-gather.2.cloned.1.call-done
  242.3 26.0 %fusion.73.clone.5 = bf16[512,4096]{1,0:T(8,128)(2,1)S(1)} fusion(bf16[1024,8192]{1,0:T(8,128)(2,1)} %all-gather.2.cloned.1.call-done, f32[512,1024]{1,0:T(8,128)} %copy-done.1, f32[1024]{0:T(1024)S(1)} %copy-done.6, f32[1024]{0:T(1024)S(1)} %copy-done.7, f32[512]{0:T(512)S(1)} %add_rsqrt_fusion.1, ...), kind=kOutput, calls=%fused_computation.24.clone.clone.clone.clone.clone.clone.2 | convolution fusion | flops 4433903616 | bytes 14692352 | tf_op jit(solution)/shard_map/dot_general | solution.py:99
  268.3 7.9 %fusion.132 = (f32[512]{0:T(512)S(1)}, f32[512,1024]{1,0:T(8,128)S(1)}) fusion(f32[1024]{0:T(1024)S(1)} %copy-done.6, f32[1024]{0:T(1024)S(1)} %copy-done.7, f32[512]{0:T(512)S(1)} %add_rsqrt_fusion.1, f32[512,1024]{1,0:T(8,128)S(1)} %copy-done.2, f32[512]{0:T(512)S(1)} %broadcast_multiply_fusion.1, bf16[1024,8192]{1,0:T(8,128)(2,1)} %all-gather.2.cloned.1.call-done, ...), kind=kOutput, calls=%fused_computation.147 | convolution fusion | flops 4299161088 | bytes 16791552 | tf_op jit(solution)/shard_map/dot_general | solution.py:104
  276.2 0.3 multiply_reduce_fusion.1
  276.6 1.5 multiply_reduce_fusion
  278.1 0.6 broadcast_in_dim.32
  278.7 3.3 %all-to-all-start.3 = ((f32[8,1,1024]{2,1,0:T(1,128)}), f32[8,1,1024]{2,1,0:T(1,128)S(1)}, u32[]{:S(2)}, u32[]{:S(2)}) async-start(f32[8,1,1024]{2,1,0:T(1,128)} %broadcast_in_dim.32), calls=%async_computation.3 | async-start | bytes 65536 | tf_op jit(solution)/shard_map/all_to_all | solution.py:45
  282.1 0.1 multiply_reduce_fusion.3
  282.2 5.2 %all-to-all-done.3 = f32[8,1,1024]{2,1,0:T(1,128)S(1)} async-done(((f32[8,1,1024]{2,1,0:T(1,128)}), f32[8,1,1024]{2,1,0:T(1,128)S(1)}, u32[]{:S(2)}, u32[]{:S(2)}) %all-to-all-start.3) | async-done | bytes 32800 | tf_op jit(solution)/shard_map/all_to_all | solution.py:45
  287.5 0.6 multiply_reduce_fusion.4
  288.8 0.6 fusion.123
  289.4 0.5 broadcast.121
  289.9 0.8 reduce.1
  290.8 0.6 reshape.80
  291.4 6.9 %all-to-all-start.4 = ((bf16[16,2,512]{2,1,0:T(2,128)(2,1)}), bf16[16,2,512]{2,1,0:T(2,128)(2,1)S(1)}, u32[]{:S(2)}, u32[]{:S(2)}) async-start(bf16[16,2,512]{2,1,0:T(2,128)(2,1)} %reshape.80), calls=%async_computation.4 | async-start | bytes 65536 | tf_op jit(solution)/shard_map/all_to_all | solution.py:45
  298.3 7.6 %all-to-all-done.4 = bf16[16,2,512]{2,1,0:T(2,128)(2,1)S(1)} async-done(((bf16[16,2,512]{2,1,0:T(2,128)(2,1)}), bf16[16,2,512]{2,1,0:T(2,128)(2,1)S(1)}, u32[]{:S(2)}, u32[]{:S(2)}) %all-to-all-start.4) | async-done | bytes 32800 | tf_op jit(solution)/shard_map/all_to_all | solution.py:45
  306.0 0.3 exponential_reduce_fusion
  306.3 0.5 log_subtract_fusion
  (29 shorter events, 0.2 us)
Async XLA Ops:
  7.2 230.4 %copy-start = (bf16[1024,1024]{1,0:T(8,128)(2,1)S(1)}, bf16[1024,1024]{1,0:T(8,128)(2,1)}, u32[]{:S(2)}) copy-start(bf16[1024,1024]{1,0:T(8,128)(2,1)} %param.17) | copy-start | bytes 6291460
  7.2 235.0 %all-gather.2.cloned.1.call-start = ((), (), s32[]{:S(2)}) async-start(), calls=%async_computation.5 | async-start | bytes 17825792 | tf_op jit(solution)/shard_map/all_gather | solution.py:13
  46.2 25.9 %all-to-all-start.1 = ((bf16[8,256,3,128]{3,1,2,0:T(8,128)(2,1)}), bf16[8,256,3,128]{3,1,2,0:T(8,128)(2,1)}, u32[]{:S(2)}, u32[]{:S(2)}) async-start(bf16[8,256,3,128]{3,1,2,0:T(8,128)(2,1)} %get-tuple-element.89), calls=%async_computation.1 | async-start | bytes 3145728 | tf_op jit(solution)/shard_map/all_to_all | solution.py:39
  216.7 25.5 %copy-start.6 = (f32[1024]{0:T(1024)S(1)}, f32[1024]{0:T(1024)}, u32[]{:S(2)}) copy-start(f32[1024]{0:T(1024)} %param.19) | copy-start | bytes 12292
  216.7 25.5 %copy-start.7 = (f32[1024]{0:T(1024)S(1)}, f32[1024]{0:T(1024)}, u32[]{:S(2)}) copy-start(f32[1024]{0:T(1024)} %param.18) | copy-start | bytes 12292
  216.7 19.6 %all-to-all-start.2 = ((bf16[8,512,128]{2,1,0:T(8,128)(2,1)}), bf16[8,512,128]{2,1,0:T(8,128)(2,1)S(1)}, u32[]{:S(2)}, u32[]{:S(2)}) async-start(bf16[8,512,128]{2,1,0:T(8,128)(2,1)} %bitcast.57), calls=%async_computation.2 | async-start | bytes 2097152 | tf_op jit(solution)/shard_map/all_to_all | solution.py:134
  240.5 1.4 copy-start.1
  242.2 26.0 %copy-start.2 = (f32[512,1024]{1,0:T(8,128)S(1)}, f32[512,1024]{1,0:T(8,128)}, u32[]{:S(2)}) copy-start(f32[512,1024]{1,0:T(8,128)} %copy-done.1) | copy-start | bytes 6291460
  268.2 8.3 %copy-start.4 = (f32[1024]{0:T(1024)S(1)}, f32[1024]{0:T(1024)}, u32[]{:S(2)}) copy-start(f32[1024]{0:T(1024)} %param.23) | copy-start | bytes 12292
  268.3 8.3 %copy-start.5 = (f32[1024]{0:T(1024)S(1)}, f32[1024]{0:T(1024)}, u32[]{:S(2)}) copy-start(f32[1024]{0:T(1024)} %param.22) | copy-start | bytes 12292
  268.3 13.8 %copy-start.3 = (f32[8,1024]{1,0:T(8,128)S(1)}, f32[8,1024]{1,0:T(8,128)}, u32[]{:S(2)}) copy-start(f32[8,1024]{1,0:T(8,128)} %param.24) | copy-start | bytes 98308
  268.3 37.7 %copy-start.8 = (s32[8]{0:T(128)S(1)}, s32[8]{0:T(128)}, u32[]{:S(2)}) copy-start(s32[8]{0:T(128)} %param.25) | copy-start | bytes 100
  278.7 8.7 %all-to-all-start.3 = ((f32[8,1,1024]{2,1,0:T(1,128)}), f32[8,1,1024]{2,1,0:T(1,128)S(1)}, u32[]{:S(2)}, u32[]{:S(2)}) async-start(f32[8,1,1024]{2,1,0:T(1,128)} %broadcast_in_dim.32), calls=%async_computation.3 | async-start | bytes 65536 | tf_op jit(solution)/shard_map/all_to_all | solution.py:45
  291.4 14.5 %all-to-all-start.4 = ((bf16[16,2,512]{2,1,0:T(2,128)(2,1)}), bf16[16,2,512]{2,1,0:T(2,128)(2,1)S(1)}, u32[]{:S(2)}, u32[]{:S(2)}) async-start(bf16[16,2,512]{2,1,0:T(2,128)(2,1)} %reshape.80), calls=%async_computation.4 | async-start | bytes 65536 | tf_op jit(solution)/shard_map/all_to_all | solution.py:45
Sparse Core Ops, SparseCore 0:
  10.1 113.5 all-gather.1
where the time goes:
time: 314 us
  matrix products  167 us (53%)
  waiting for transfers between devices  49.4 us (16%)
  blocking collectives  26.9 us (9%)
  local copies, waits for them, and re-layouts  21.2 us (7%)
  starting transfers between devices  18.5 us (6%)
  between operations  15.6 us (5%)
  other arithmetic  12.1 us (4%)
    sub x4, matrix products, one_block(): expo = jnp.exp(scores - highest)  68.8 us
    dot_general x4, matrix products, one_block(): jnp.einsum('hqk,khd->qhd', probs, value_all, preferred_element_type=jnp.f...  54.7 us
    all_to_all x1, blocking collectives, several_exchanges(): lax.all_to_all(slab, axis, split_axis=0, concat_axis=0, tiled=True)  26.9 us
    dot_general x1, matrix products, expand_inner(): jnp.dot(rows_in, up_full, preferred_element_type=jnp.float32)  26 us
    all_to_all x1, waiting for transfers between devices, several_exchanges(): lax.all_to_all(slab, axis, split_axis=0, concat_axis=0, tiled=True)  21.4 us
    all_to_all x1, waiting for transfers between devices, body(): lax.all_to_all(attended, 'seq', split_axis=0, concat_axis=1, tiled=True)  15.2 us
    all_to_all x2, waiting for transfers between devices, sent_to_all(): return lax.all_to_all(copies, axis, split_axis=0, concat_axis=0, tiled=True)  12.8 us
    all_to_all x2, starting transfers between devices, sent_to_all(): return lax.all_to_all(copies, axis, split_axis=0, concat_axis=0, tiled=True)  10.3 us
  transfers between devices with their start and end apart: 5, of which 4 were waited for; matrix products, arithmetic and copies ran while one was open for 50% of the time, Pallas kernels for 0%

commit v1 on v0

--- a/solution.py
+++ b/solution.py
@@ -131,7 +131,10 @@
     projected = projected.reshape(tok_rows, 3, width)
     gathered = several_exchanges(projected, "seq", 2, 2, 0)
     attended = attend_local(gathered, length)
-    returned = lax.all_to_all(attended, "seq", split_axis=0, concat_axis=1, tiled=True)
+    returned = jnp.concatenate(
+        lax.all_to_all(jnp.stack(jnp.split(attended, lax.axis_size("seq"), axis=0)), "seq", 0, 0),
+        axis=1,
+    )
     mixed = jnp.dot(returned, output_weight, preferred_element_type=jnp.float32)
     mixed = mixed + tokens.astype(jnp.float32)
     normed = layer_norm(mixed, first_gain, first_shift).astype(jnp.bfloat16)

time: 314 us -> 327 us (1.041)
  local copies, waits for them, and re-layouts: 21.2 us -> 33.7 us
    unnamed x21 -> x28, local copies, waits for them, and re-layouts: 2.88 us -> 13.8 us
  transfers between devices with their start and end apart: 5 -> 5, of which waited for: 4 -> 4; matrix products, arithmetic and copies ran while one was open for 50% -> 52% of each run, Pallas kernels for 0% -> 0%
where the time goes in v1:
time: 327 us; the launch traced here: 326 us
  matrix products  167 us (51%)
  waiting for transfers between devices  49.4 us (15%)
  local copies, waits for them, and re-layouts  33.7 us (10%)
  blocking collectives  26.9 us (8%)
  starting transfers between devices  18.3 us (6%)
  between operations  15.6 us (5%)
  other arithmetic  12.1 us (4%)
    sub x4, matrix products, one_block(): expo = jnp.exp(scores - highest)  68.8 us
    dot_general x4, matrix products, one_block(): jnp.einsum('hqk,khd->qhd', probs, value_all, preferred_element_type=jnp.f...  54.7 us
    all_to_all x1, blocking collectives, several_exchanges(): lax.all_to_all(slab, axis, split_axis=0, concat_axis=0, tiled=True)  26.9 us
    dot_general x1, matrix products, expand_inner(): jnp.dot(rows_in, up_full, preferred_element_type=jnp.float32)  26 us
    all_to_all x1, waiting for transfers between devices, several_exchanges(): lax.all_to_all(slab, axis, split_axis=0, concat_axis=0, tiled=True)  21.4 us
    all_to_all x1, waiting for transfers between devices, body(): lax.all_to_all(jnp.stack(jnp.split(attended, lax.axis_size('seq'), axis=0...  15.2 us
    unnamed x28, local copies, waits for them, and re-layouts  13.8 us
    all_to_all x2, waiting for transfers between devices, sent_to_all(): return lax.all_to_all(copies, axis, split_axis=0, concat_axis=0, tiled=True)  12.8 us
  transfers between devices with their start and end apart: 5, of which 4 were waited for; matrix products, arithmetic and copies ran while one was open for 52% of the time, Pallas kernels for 0%

profile of v1, /device:TPU:0, one launch (start us, length us, event | category | flops | bytes accessed | tf_op | source)
XLA Modules:
  0.0 326.1 jit_solution(12555600392749249684)
XLA Ops:
  7.2 2.4 pad_maximum_fusion.1
  9.6 6.6 %fusion.69 = bf16[64,8,24,128]{3,1,2,0:T(8,128)(2,1)S(1)} fusion(bf16[1024,3072]{1,0:T(8,128)(2,1)} %param.16, bf16[1,512,1024]{2,1,0:T(8,128)(2,1)} %param.14), kind=kOutput, calls=%fused_computation.84 | convolution fusion | flops 3222798336 | bytes 10485760 | tf_op jit(solution)/shard_map/dot_general | solution.py:128
  16.2 0.9 copy.57
  17.1 0.7 copy.65
  17.7 1.5 fusion.138
  19.3 26.9 %all_to_all.26 = bf16[8,256,3,128]{3,1,2,0:T(8,128)(2,1)} all-to-all(bf16[8,256,3,128]{3,1,2,0:T(8,128)(2,1)S(1)} %get-tuple-element.88), channel_id=1, replica_groups=mesh['seq'=8,'grp'=16] {'seq'}, dimensions={0} | all-to-all | bytes 3145728 | tf_op jit(solution)/shard_map/all_to_all | solution.py:39
  46.2 4.5 %all-to-all-start.1 = ((bf16[8,256,3,128]{3,1,2,0:T(8,128)(2,1)}), bf16[8,256,3,128]{3,1,2,0:T(8,128)(2,1)}, u32[]{:S(2)}, u32[]{:S(2)}) async-start(bf16[8,256,3,128]{3,1,2,0:T(8,128)(2,1)} %get-tuple-element.89), calls=%async_computation.1 | async-start | bytes 3145728 | tf_op jit(solution)/shard_map/all_to_all | solution.py:39
  50.6 21.4 %all-to-all-done.1 = bf16[8,256,3,128]{3,1,2,0:T(8,128)(2,1)} async-done(((bf16[8,256,3,128]{3,1,2,0:T(8,128)(2,1)}), bf16[8,256,3,128]{3,1,2,0:T(8,128)(2,1)}, u32[]{:S(2)}, u32[]{:S(2)}) %all-to-all-start.1) | async-done | bytes 1572896 | tf_op jit(solution)/shard_map/all_to_all | solution.py:39
  72.0 2.2 pad_maximum_fusion
  74.5 1.6 fusion.137
  76.1 2.3 copy.46
  78.4 2.3 copy.47
  80.7 1.3 copy.48
  82.0 134.7 %while.11 = (s32[]{:T(128)}, bf16[4,1024,128]{2,1,0:T(8,128)(2,1)}, s32[4]{0:T(128)S(1)}, bf16[4096,2,64]{0,2,1:T(8,128)(2,1)}, bf16[4096,2,64]{0,2,1:T(8,128)(2...) while((s32[]{:T(128)}, bf16[4,1024,128]{2,1,0:T(8,128)(2,1)}, ...), condition=%wide.region_3.4_spmd.clone, body=%wide.region_0.3_spmd.clone.sunk | while | flops 2197954560 | bytes 70804144 | solution.py:89
  82.0 0.6 dynamic_slice.24
  83.2 0.7 iota_compare_fusion.3
  83.9 17.5 %fusion.162 = (f32[2,1024]{1,0:T(2,128)S(1)}, f32[2,1024,4096]{2,1,0:T(8,128)}) fusion(pred[4096]{0:T(1024)(128)(4,1)S(1)} %iota_compare_fusion.3, bf16[4096,2,64]{0,2,1:T(8,128)(2,1)} %get-tuple-element.169, bf16[4096,2,64]{0,2,1:T(8,128)(2,1)} %get-tuple-element.168, s32[]{:T(128)S(6)} %select_n.28), kind=kOutput, calls=%fused_computation.159.clone.1 | convolution fusion | flops 1107300352 | bytes 34877444 | tf_op jit(solution)/shard_map/while/body/eval_jaxpr/sub | solution.py:84
  101.4 13.9 %fusion.163 = bf16[2,1024,64]{1,2,0:T(8,128)(2,1)S(1)} fusion(bf16[4096,2,64]{0,2,1:T(8,128)(2,1)} %get-tuple-element.170, f32[2,1024,4096]{2,1,0:T(8,128)} %get-tuple-element.141, f32[2,1024]{1,0:T(2,128)S(1)} %get-tuple-element.142), kind=kOutput, calls=%fused_computation.11.clone.1 | convolution fusion | flops 1090650112 | bytes 34873344 | tf_op jit(solution)/shard_map/while/body/eval_jaxpr/hqk,khd->qhd/dot_general | solution.py:86
  115.5 0.7 constant_dynamic-update-slice_fusion.2
  116.2 0.6 dynamic_slice.24
  117.5 0.7 iota_compare_fusion.3
  118.1 17.1 %fusion.162 = (f32[2,1024]{1,0:T(2,128)S(1)}, f32[2,1024,4096]{2,1,0:T(8,128)}) fusion(pred[4096]{0:T(1024)(128)(4,1)S(1)} %iota_compare_fusion.3, bf16[4096,2,64]{0,2,1:T(8,128)(2,1)} %get-tuple-element.169, bf16[4096,2,64]{0,2,1:T(8,128)(2,1)} %get-tuple-element.168, s32[]{:T(128)S(6)} %select_n.28), kind=kOutput, calls=%fused_computation.159.clone.1 | convolution fusion | flops 1107300352 | bytes 34877444 | tf_op jit(solution)/shard_map/while/body/eval_jaxpr/sub | solution.py:84
  135.2 13.6 %fusion.163 = bf16[2,1024,64]{1,2,0:T(8,128)(2,1)S(1)} fusion(bf16[4096,2,64]{0,2,1:T(8,128)(2,1)} %get-tuple-element.170, f32[2,1024,4096]{2,1,0:T(8,128)} %get-tuple-element.141, f32[2,1024]{1,0:T(2,128)S(1)} %get-tuple-element.142), kind=kOutput, calls=%fused_computation.11.clone.1 | convolution fusion | flops 1090650112 | bytes 34873344 | tf_op jit(solution)/shard_map/while/body/eval_jaxpr/hqk,khd->qhd/dot_general | solution.py:86
  149.0 0.7 constant_dynamic-update-slice_fusion.2
  149.7 0.6 dynamic_slice.24
  151.0 0.7 iota_compare_fusion.3
  151.6 17.1 %fusion.162 = (f32[2,1024]{1,0:T(2,128)S(1)}, f32[2,1024,4096]{2,1,0:T(8,128)}) fusion(pred[4096]{0:T(1024)(128)(4,1)S(1)} %iota_compare_fusion.3, bf16[4096,2,64]{0,2,1:T(8,128)(2,1)} %get-tuple-element.169, bf16[4096,2,64]{0,2,1:T(8,128)(2,1)} %get-tuple-element.168, s32[]{:T(128)S(6)} %select_n.28), kind=kOutput, calls=%fused_computation.159.clone.1 | convolution fusion | flops 1107300352 | bytes 34877444 | tf_op jit(solution)/shard_map/while/body/eval_jaxpr/sub | solution.py:84
  168.7 13.6 %fusion.163 = bf16[2,1024,64]{1,2,0:T(8,128)(2,1)S(1)} fusion(bf16[4096,2,64]{0,2,1:T(8,128)(2,1)} %get-tuple-element.170, f32[2,1024,4096]{2,1,0:T(8,128)} %get-tuple-element.141, f32[2,1024]{1,0:T(2,128)S(1)} %get-tuple-element.142), kind=kOutput, calls=%fused_computation.11.clone.1 | convolution fusion | flops 1090650112 | bytes 34873344 | tf_op jit(solution)/shard_map/while/body/eval_jaxpr/hqk,khd->qhd/dot_general | solution.py:86
  182.5 0.7 constant_dynamic-update-slice_fusion.2
  183.2 0.6 dynamic_slice.24
  184.5 0.7 iota_compare_fusion.3
  185.1 17.1 %fusion.162 = (f32[2,1024]{1,0:T(2,128)S(1)}, f32[2,1024,4096]{2,1,0:T(8,128)}) fusion(pred[4096]{0:T(1024)(128)(4,1)S(1)} %iota_compare_fusion.3, bf16[4096,2,64]{0,2,1:T(8,128)(2,1)} %get-tuple-element.169, bf16[4096,2,64]{0,2,1:T(8,128)(2,1)} %get-tuple-element.168, s32[]{:T(128)S(6)} %select_n.28), kind=kOutput, calls=%fused_computation.159.clone.1 | convolution fusion | flops 1107300352 | bytes 34877444 | tf_op jit(solution)/shard_map/while/body/eval_jaxpr/sub | solution.py:84
  202.2 13.6 %fusion.163 = bf16[2,1024,64]{1,2,0:T(8,128)(2,1)S(1)} fusion(bf16[4096,2,64]{0,2,1:T(8,128)(2,1)} %get-tuple-element.170, f32[2,1024,4096]{2,1,0:T(8,128)} %get-tuple-element.141, f32[2,1024]{1,0:T(2,128)S(1)} %get-tuple-element.142), kind=kOutput, calls=%fused_computation.11.clone.1 | convolution fusion | flops 1090650112 | bytes 34873344 | tf_op jit(solution)/shard_map/while/body/eval_jaxpr/hqk,khd->qhd/dot_general | solution.py:86
  216.0 0.7 constant_dynamic-update-slice_fusion.2
  216.7 1.6 fusion.96
  218.3 1.6 fusion.95
  219.9 1.6 fusion.94
  221.4 1.6 fusion.93
  223.0 1.6 fusion.92
  224.6 1.5 fusion.91
  226.1 1.6 fusion.90
  227.7 1.6 fusion.89
  229.3 3.6 %all-to-all-start.2 = ((bf16[8,512,128]{2,1,0:T(8,128)(2,1)}), bf16[8,512,128]{2,1,0:T(8,128)(2,1)S(1)}, u32[]{:S(2)}, u32[]{:S(2)}) async-start(bf16[8,512,128]{2,1,0:T(8,128)(2,1)} %fusion.89), calls=%async_computation.2 | async-start | bytes 2097152 | tf_op jit(solution)/shard_map/all_to_all | solution.py:135
  233.5 15.2 %all-to-all-done.2 = bf16[8,512,128]{2,1,0:T(8,128)(2,1)S(1)} async-done(((bf16[8,512,128]{2,1,0:T(8,128)(2,1)}), bf16[8,512,128]{2,1,0:T(8,128)(2,1)S(1)}, u32[]{:S(2)}, u32[]{:S(2)}) %all-to-all-start.2) | async-done | bytes 1048608 | tf_op jit(solution)/shard_map/all_to_all | solution.py:135
  248.7 1.3 copy.50
  250.0 2.9 fusion.139
  252.9 1.3 copy-done.1
  254.2 0.3 multiply_reduce_fusion.2
  254.6 26.0 %fusion.73.clone.5 = bf16[512,4096]{1,0:T(8,128)(2,1)S(1)} fusion(bf16[1024,8192]{1,0:T(8,128)(2,1)} %all-gather.2.cloned.1.call-done, f32[512,1024]{1,0:T(8,128)} %copy-done.1, f32[1024]{0:T(1024)S(1)} %copy-done.6, f32[1024]{0:T(1024)S(1)} %copy-done.7, f32[512]{0:T(512)S(1)} %add_rsqrt_fusion.1, ...), kind=kOutput, calls=%fused_computation.24.clone.clone.clone.clone.clone.clone.2 | convolution fusion | flops 4433903616 | bytes 14692352 | tf_op jit(solution)/shard_map/dot_general | solution.py:99
  280.7 7.9 %fusion.140 = (f32[512]{0:T(512)S(1)}, f32[512,1024]{1,0:T(8,128)S(1)}) fusion(f32[1024]{0:T(1024)S(1)} %copy-done.6, f32[1024]{0:T(1024)S(1)} %copy-done.7, f32[512]{0:T(512)S(1)} %add_rsqrt_fusion.1, f32[512,1024]{1,0:T(8,128)S(1)} %copy-done.2, f32[512]{0:T(512)S(1)} %broadcast_multiply_fusion.1, bf16[1024,8192]{1,0:T(8,128)(2,1)} %all-gather.2.cloned.1.call-done, ...), kind=kOutput, calls=%fused_computation.163 | convolution fusion | flops 4299161088 | bytes 16791552 | tf_op jit(solution)/shard_map/dot_general | solution.py:104
  288.6 0.3 multiply_reduce_fusion.1
  289.0 1.5 multiply_reduce_fusion
  290.5 0.6 broadcast_in_dim.32
  291.1 3.3 %all-to-all-start.3 = ((f32[8,1,1024]{2,1,0:T(1,128)}), f32[8,1,1024]{2,1,0:T(1,128)S(1)}, u32[]{:S(2)}, u32[]{:S(2)}) async-start(f32[8,1,1024]{2,1,0:T(1,128)} %broadcast_in_dim.32), calls=%async_computation.3 | async-start | bytes 65536 | tf_op jit(solution)/shard_map/all_to_all | solution.py:45
  294.6 5.2 %all-to-all-done.3 = f32[8,1,1024]{2,1,0:T(1,128)S(1)} async-done(((f32[8,1,1024]{2,1,0:T(1,128)}), f32[8,1,1024]{2,1,0:T(1,128)S(1)}, u32[]{:S(2)}, u32[]{:S(2)}) %all-to-all-start.3) | async-done | bytes 32800 | tf_op jit(solution)/shard_map/all_to_all | solution.py:45
  299.9 0.6 multiply_reduce_fusion.4
  301.2 0.6 fusion.131
  301.8 0.5 broadcast.121
  302.3 0.8 reduce.1
  303.1 0.6 reshape.87
  303.8 6.9 %all-to-all-start.4 = ((bf16[16,2,512]{2,1,0:T(2,128)(2,1)}), bf16[16,2,512]{2,1,0:T(2,128)(2,1)S(1)}, u32[]{:S(2)}, u32[]{:S(2)}) async-start(bf16[16,2,512]{2,1,0:T(2,128)(2,1)} %reshape.87), calls=%async_computation.4 | async-start | bytes 65536 | tf_op jit(solution)/shard_map/all_to_all | solution.py:45
  310.7 7.6 %all-to-all-done.4 = bf16[16,2,512]{2,1,0:T(2,128)(2,1)S(1)} async-done(((bf16[16,2,512]{2,1,0:T(2,128)(2,1)}), bf16[16,2,512]{2,1,0:T(2,128)(2,1)S(1)}, u32[]{:S(2)}, u32[]{:S(2)}) %all-to-all-start.4) | async-done | bytes 32800 | tf_op jit(solution)/shard_map/all_to_all | solution.py:45
  318.3 0.3 exponential_reduce_fusion
  318.7 0.5 log_subtract_fusion
  (37 shorter events, 1.3 us)
Async XLA Ops:
  7.2 242.8 %copy-start = (bf16[1024,1024]{1,0:T(8,128)(2,1)S(1)}, bf16[1024,1024]{1,0:T(8,128)(2,1)}, u32[]{:S(2)}) copy-start(bf16[1024,1024]{1,0:T(8,128)(2,1)} %param.17) | copy-start | bytes 6291460
  7.2 247.4 %all-gather.2.cloned.1.call-start = ((), (), s32[]{:S(2)}) async-start(), calls=%async_computation.5 | async-start | bytes 17825792 | tf_op jit(solution)/shard_map/all_gather | solution.py:13
  46.2 25.9 %all-to-all-start.1 = ((bf16[8,256,3,128]{3,1,2,0:T(8,128)(2,1)}), bf16[8,256,3,128]{3,1,2,0:T(8,128)(2,1)}, u32[]{:S(2)}, u32[]{:S(2)}) async-start(bf16[8,256,3,128]{3,1,2,0:T(8,128)(2,1)} %get-tuple-element.89), calls=%async_computation.1 | async-start | bytes 3145728 | tf_op jit(solution)/shard_map/all_to_all | solution.py:39
  216.7 37.9 %copy-start.6 = (f32[1024]{0:T(1024)S(1)}, f32[1024]{0:T(1024)}, u32[]{:S(2)}) copy-start(f32[1024]{0:T(1024)} %param.19) | copy-start | bytes 12292
  216.7 37.9 %copy-start.7 = (f32[1024]{0:T(1024)S(1)}, f32[1024]{0:T(1024)}, u32[]{:S(2)}) copy-start(f32[1024]{0:T(1024)} %param.18) | copy-start | bytes 12292
  229.3 19.4 %all-to-all-start.2 = ((bf16[8,512,128]{2,1,0:T(8,128)(2,1)}), bf16[8,512,128]{2,1,0:T(8,128)(2,1)S(1)}, u32[]{:S(2)}, u32[]{:S(2)}) async-start(bf16[8,512,128]{2,1,0:T(8,128)(2,1)} %fusion.89), calls=%async_computation.2 | async-start | bytes 2097152 | tf_op jit(solution)/shard_map/all_to_all | solution.py:135
  252.9 1.4 copy-start.1
  254.6 26.0 %copy-start.2 = (f32[512,1024]{1,0:T(8,128)S(1)}, f32[512,1024]{1,0:T(8,128)}, u32[]{:S(2)}) copy-start(f32[512,1024]{1,0:T(8,128)} %copy-done.1) | copy-start | bytes 6291460
  280.6 8.3 %copy-start.4 = (f32[1024]{0:T(1024)S(1)}, f32[1024]{0:T(1024)}, u32[]{:S(2)}) copy-start(f32[1024]{0:T(1024)} %param.23) | copy-start | bytes 12292
  280.6 8.3 %copy-start.5 = (f32[1024]{0:T(1024)S(1)}, f32[1024]{0:T(1024)}, u32[]{:S(2)}) copy-start(f32[1024]{0:T(1024)} %param.22) | copy-start | bytes 12292
  280.7 13.8 %copy-start.3 = (f32[8,1024]{1,0:T(8,128)S(1)}, f32[8,1024]{1,0:T(8,128)}, u32[]{:S(2)}) copy-start(f32[8,1024]{1,0:T(8,128)} %param.24) | copy-start | bytes 98308
  280.7 37.7 %copy-start.8 = (s32[8]{0:T(128)S(1)}, s32[8]{0:T(128)}, u32[]{:S(2)}) copy-start(s32[8]{0:T(128)} %param.25) | copy-start | bytes 100
  291.1 8.7 %all-to-all-start.3 = ((f32[8,1,1024]{2,1,0:T(1,128)}), f32[8,1,1024]{2,1,0:T(1,128)S(1)}, u32[]{:S(2)}, u32[]{:S(2)}) async-start(f32[8,1,1024]{2,1,0:T(1,128)} %broadcast_in_dim.32), calls=%async_computation.3 | async-start | bytes 65536 | tf_op jit(solution)/shard_map/all_to_all | solution.py:45
  303.8 14.5 %all-to-all-start.4 = ((bf16[16,2,512]{2,1,0:T(2,128)(2,1)}), bf16[16,2,512]{2,1,0:T(2,128)(2,1)S(1)}, u32[]{:S(2)}, u32[]{:S(2)}) async-start(bf16[16,2,512]{2,1,0:T(2,128)(2,1)} %reshape.87), calls=%async_computation.4 | async-start | bytes 65536 | tf_op jit(solution)/shard_map/all_to_all | solution.py:45
Sparse Core Ops, SparseCore 0:
  10.1 113.5 all-gather.1
